TPU v7x, 32 devices: a whole 2x2x4 slice. The times are simulated.
32 devices in a mesh: dp: 4 (over y, core), vocab: 8 (over z, x).
Axes of the slice: x: 2, y: 2, z: 4, core: 2. Of those that a mesh axis runs over, the one named last changes fastest.
Arguments:
- hidden: bfloat16 [768, 8192], P('dp', 'vocab'), may hold values from -100 to 100
- proj: bfloat16 [8192, 65536], P(None, ('dp', 'vocab')), may hold values from -3 to 3
- target_ids: int32 [768], replicated, may hold values from 0 to 65535
- seq_len: int32 [16], replicated, may hold values from 1 to 189, as said below
- seq_way: int32 [16], replicated, may hold values from 0 to 3
Outputs:
- token_logprob: float32 [768], P('dp')
- token_entropy: float32 [768], P('dp')
- seq_logprob: float32 [16], replicated
Inputs may be any that keep to these rules, and one draw needn't show every extreme that they name: `seq_len`: each data way is given exactly 4 sequences, which fill its first slots one after another in increasing sequence number; the lengths on one way add up to at most 192, to exactly 192 on some way, and over all ways to exactly 372. Some sequence has exactly 189 tokens.
All inputs are finite; a program needn't handle non-finite values.
Results may differ from a plain program's by a relative error of at most 0.0003.
Values may be sent and summed in bfloat16 or wider, within the bound.
No kernel may reach another device: no remote copies, remote signals or barrier semaphores. Data moves between devices by JAX's collectives and lax.ppermute only.
A program may use at most 128 MiB of HBM per device.

v0:
```python
import jax
import jax.numpy as jnp
from jax import lax
from jax.sharding import PartitionSpec as P


def membership(seq_len, seq_way, slots, ways):
    count = seq_len.shape[0]
    order = jnp.arange(count, dtype=jnp.int32)
    earlier = (seq_way[:, None] == seq_way[None, :]) & (order[:, None] < order[None, :])
    start = jnp.sum(jnp.where(earlier, seq_len[:, None], 0), axis=0)
    row = jnp.arange(slots * ways, dtype=jnp.int32)
    owner = row // slots
    within = row % slots
    return (
        (seq_way[None, :] == owner[:, None])
        & (within[:, None] >= start[None, :])
        & (within[:, None] < (start + seq_len)[None, :])
    )


def target_logit(logits, first_col, targets):
    columns = first_col + jnp.arange(logits.shape[1], dtype=jnp.int32)
    return jnp.sum(jnp.where(targets[:, None] == columns[None, :], logits, 0.0), axis=1)


def per_device(hidden, proj, target_ids, seq_len, seq_way):
    ways = lax.axis_size("dp")
    slots = hidden.shape[0]
    width = proj.shape[1]
    first_col = (lax.axis_index("dp") * lax.axis_size("vocab") + lax.axis_index("vocab")) * width
    member = membership(seq_len, seq_way, slots, ways)
    valid = jnp.any(member, axis=1)
    kept = slots + (ways - 1) * (5 * slots // 16)
    source = jnp.nonzero(valid, size=kept)[0].astype(jnp.int32)
    slot_rows = lax.all_gather(hidden, "dp", axis=0, tiled=True)
    slot_rows = jnp.take(slot_rows, source, axis=0)
    empty = jnp.zeros((slot_rows.shape[0], width), jnp.float32)
    piece = lax.all_gather(slot_rows, "vocab", axis=1, tiled=True)
    weights_part = lax.slice_in_dim(proj, 0, piece.shape[1], axis=0)
    logits = empty + jnp.dot(piece, weights_part, preferred_element_type=jnp.float32)
    targets = jnp.take(target_ids, source)
    top = lax.pmax(jnp.max(logits, axis=1), ("dp", "vocab"))
    shifted = logits - top[:, None]
    weight = jnp.exp(shifted)
    partial_total = jnp.sum(weight, axis=1)
    partial_moment = jnp.sum(weight * shifted, axis=1)
    partial_pick = target_logit(logits, first_col, targets)
    total, moment, picked = lax.psum((partial_total, partial_moment, partial_pick), ("dp", "vocab"))
    log_total = jnp.log(total)
    logprob = picked - top - log_total
    entropy = log_total - moment / total
    position = jnp.clip(jnp.cumsum(valid.astype(jnp.int32)) - 1, 0, kept - 1)
    logprob = jnp.take(logprob, position)
    entropy = jnp.take(entropy, position)
    logprob = jnp.where(valid, logprob, 0.0)
    entropy = jnp.where(valid, entropy, 0.0)
    seq_logprob = jnp.dot(member.astype(jnp.float32).T, logprob, precision=lax.Precision.HIGHEST)
    mine = lax.axis_index("dp") * slots
    return (
        lax.dynamic_slice_in_dim(logprob, mine, slots),
        lax.dynamic_slice_in_dim(entropy, mine, slots),
        seq_logprob,
    )


def solution(mesh):
    placed = (P("dp", "vocab"), P(None, ("dp", "vocab")), P(), P(), P())
    return jax.shard_map(
        per_device, mesh=mesh, in_specs=placed, out_specs=(P("dp"), P("dp"), P()), check_vma=False
    )
```

profile of v0, /device:TPU:0, one launch (start us, length us, event | category | flops | bytes accessed | tf_op | source)
XLA Modules:
  0.0 252.8 jit_solution(5199935121972603821)
XLA Ops:
  7.2 0.0 copy-start
  7.2 0.0 all-gather.3.cloned.1.call-start
  7.2 0.7 all-gather.3.cloned.1.call-update
  7.9 0.0 all-gather.5.cloned.1.call-start
  8.0 0.8 select_reduce_fusion.1
  8.8 0.7 add.90
  9.4 0.8 and_reduce_fusion
  10.2 0.3 reduce-window.16
  10.5 0.1 slice.15
  10.6 0.1 slice_reduce_fusion
  10.7 0.1 add_bitcast_fusion
  10.8 5.8 %scatter_custom_fusion = s32[372]{0:T(512)S(1)} fusion(s32[768]{0:T(1024)S(1)} %fusion.17, s32[768]{0:T(1024)S(1)} %ne.69, s32[]{:T(128)} %constant.99.clone.1), kind=kCustom, calls=%fused_computation.60 | custom fusion | flops 768 | bytes 1492 | tf_op jit(solution)/shard_map/scatter-add | solution.py:35
  16.7 0.3 reduce-window.24
  17.0 0.1 slice.17
  17.1 0.6 convert_reduce_fusion
  17.7 0.1 slice_reduce_fusion.1
  17.9 0.1 add_bitcast_fusion.1
  17.9 0.7 compare_select_fusion.2
  18.6 0.0 copy-done
  18.6 1.9 gather_fusion
  20.5 0.7 broadcast_select_fusion.1
  21.2 10.8 %all-gather.3.cloned.1.call-done = bf16[768,1024]{1,0:T(8,128)(2,1)} async-done(((bf16[192,1024]{1,0:T(8,128)(2,1)}), bf16[768,1024]{1,0:T(8,128)(2,1)}) %all-gather.3.cloned.1.call-update) | async-done | bytes 1572880 | tf_op jit(solution)/shard_map/all_gather | solution.py:36
  32.0 4.4 %gather_fusion.1 = bf16[372,1024]{1,0:T(8,128)(2,1)S(1)} fusion(bf16[768,1024]{1,0:T(8,128)(2,1)} %all-gather.3.cloned.1.call-done, s32[1024]{0:T(1024)S(1)} %pad_clamp_fusion.1), kind=kCustom, calls=%fused_computation.3 | custom fusion | bytes 1525200 | tf_op jit(solution)/shard_map/jit(_take)/gather | solution.py:37
  36.4 1.0 broadcast_select_fusion
  37.4 0.0 all-gather.5.cloned.1.call-update
  37.5 0.1 compare_select_fusion.1
  37.6 97.1 %all-gather.5.cloned.1.call-done = bf16[372,8192]{1,0:T(8,128)(2,1)} async-done(((bf16[372,1024]{1,0:T(8,128)(2,1)}), bf16[372,8192]{1,0:T(8,128)(2,1)}) %all-gather.5.cloned.1.call-update) | async-done | bytes 6094864 | tf_op jit(solution)/shard_map/all_gather | solution.py:39
  134.7 18.9 %fusion.21 = (f32[372]{0:T(512)S(1)}, f32[372,2048]{1,0:T(8,128)S(1)}) fusion(bf16[372,8192]{1,0:T(8,128)(2,1)} %all-gather.5.cloned.1.call-done, bf16[8192,2048]{1,0:T(8,128)(2,1)} %param.8), kind=kOutput, calls=%fused_computation.62 | convolution fusion | flops 12483010560 | bytes 42698192 | tf_op jit(solution)/shard_map/dot_general | solution.py:41
  153.6 38.4 %pmax.7 = f32[372]{0:T(512)S(1)} all-reduce(f32[372]{0:T(512)S(1)} %get-tuple-element.16), channel_id=1, replica_groups=mesh['dp'=4,'vocab'=8] {'dp','vocab'}, use_global_device_ids=true, to_apply=%region_11.12 | all-reduce | flops 372 | bytes 2976 | tf_op jit(solution)/shard_map/pmax | solution.py:43
  192.0 1.1 fusion
  193.1 40.8 %all-reduce.1 = (f32[372]{0:T(512)S(1)}, f32[372]{0:T(512)S(1)}, f32[372]{0:T(512)S(1)}) all-reduce(f32[372]{0:T(512)S(1)} %get-tuple-element.6, f32[372]{0:T(512)S(1)} %get-tuple-element.5, f32[372]{0:T(512)S(1)} %get-tuple-element.4), channel_id=1, replica_groups=mesh['dp'=4,'vocab'=8] {'dp','vocab'}, use_global_device_ids=true, to_apply=%region_9.10 | all-reduce | flops 1116 | bytes 8928 | tf_op jit(solution)/shard_map/psum | solution.py:49
  233.9 5.0 %gather_fusion.2 = f32[768]{0:T(1024)S(1)} fusion(f32[372]{0:T(512)S(1)} %get-tuple-element.14, s32[1024]{0:T(1024)S(1)} %pad_clamp_fusion), kind=kCustom, calls=%fused_computation.clone | custom fusion | bytes 9216 | tf_op jit(solution)/shard_map/jit(_take)/gather | solution.py:54
  238.9 0.0 copy-start.1
  238.9 5.0 %gather_fusion.3 = f32[768]{0:T(1024)S(1)} fusion(f32[372]{0:T(512)S(1)} %get-tuple-element.15, s32[1024]{0:T(1024)S(1)} %pad_clamp_fusion), kind=kCustom, calls=%fused_computation.1.clone | custom fusion | bytes 9216 | tf_op jit(solution)/shard_map/jit(_take)/gather | solution.py:55
  244.0 0.0 copy-done.1
  244.0 0.7 convolution_bitcast_fusion
  244.7 0.6 dynamic_slice.6
  245.4 0.6 dynamic_slice.7
  (14 shorter events, 0.1 us)
Async XLA Ops:
  7.2 11.5 %copy-start = (s32[768]{0:T(1024)S(1)}, s32[768]{0:T(1024)}, u32[]{:S(2)}) copy-start(s32[768]{0:T(1024)} %param.9) | copy-start | bytes 9220
  7.2 24.8 %all-gather.3.cloned.1.call-start = ((), (), s32[]{:S(2)}) async-start(), calls=%async_computation | async-start | bytes 1966080 | tf_op jit(solution)/shard_map/all_gather | solution.py:36
  7.9 126.8 %all-gather.5.cloned.1.call-start = ((), (), s32[]{:S(2)}) async-start(), calls=%async_computation.1 | async-start | bytes 6930432 | tf_op jit(solution)/shard_map/all_gather | solution.py:39
  238.9 5.1 %copy-start.1 = (s32[16]{0:T(128)S(1)}, s32[16]{0:T(128)}, u32[]{:S(2)}) copy-start(s32[16]{0:T(128)} %param.11) | copy-start | bytes 196
Sparse Core Ops, SparseCore 0:
  9.5 22.3 all-gather.2
  37.6 97.0 all-gather.4
where the time goes:
time: 253 us
  waiting for transfers between devices  109 us (43%)
  blocking collectives  79.2 us (31%)
  matrix products  19.6 us (8%)
  local copies, waits for them, and re-layouts  18 us (7%)
  between operations  14.2 us (6%)
  other arithmetic  13.1 us (5%)
    all_gather x1, waiting for transfers between devices, per_device(): piece = lax.all_gather(slot_rows, 'vocab', axis=1, tiled=True)  97.1 us
    psum x1, blocking collectives, per_device(): lax.psum((partial_total, partial_moment, partial_pick), ('dp', 'vocab'))  40.8 us
    pmax x1, blocking collectives, per_device(): top = lax.pmax(jnp.max(logits, axis=1), ('dp', 'vocab'))  38.4 us
    dot_general x1, matrix products, per_device(): jnp.dot(piece, weights_part, preferred_element_type=jnp.float32)  18.9 us
    all_gather x1, waiting for transfers between devices, per_device(): slot_rows = lax.all_gather(hidden, 'dp', axis=0, tiled=True)  10.8 us
    scatter-add x1, other arithmetic, per_device(): source = jnp.nonzero(valid, size=kept)[0].astype(jnp.int32)  5.85 us
  transfers between devices with their start and end apart: 2, of which 2 were waited for; matrix products, arithmetic and copies ran while one was open for 5% of the time, Pallas kernels for 0%

commit v1 on v0

v1 whole, which is shorter than its diff:
```python
import functools

import jax
import jax.numpy as jnp
from jax import lax
from jax.experimental import pallas as pl
from jax.experimental.pallas import tpu as pltpu
from jax.sharding import PartitionSpec as P


AXES = ("dp", "vocab")
PAIR = 2
LANES = 128
BF16, F32, I32 = jnp.bfloat16, jnp.float32, jnp.int32


def round_up(value, step):
    return -(-value // step) * step


def in_vmem():
    return pl.BlockSpec(memory_space=pltpu.VMEM)


def in_smem():
    return pl.BlockSpec(memory_space=pltpu.SMEM)


def call(kernel, operands, specs, shapes, flops, scratch=(), alias=None, mib=8):
    return pl.pallas_call(
        kernel,
        in_specs=specs,
        out_specs=jax.tree.map(lambda _: in_vmem(), shapes),
        out_shape=shapes,
        scratch_shapes=list(scratch),
        input_output_aliases=alias or {},
        compiler_params=pltpu.CompilerParams(vmem_limit_bytes=mib * 1024 * 1024),
        cost_estimate=pl.CostEstimate(flops=flops, bytes_accessed=1000000, transcendentals=0),
    )(*operands)


def array(shape, dtype):
    return jax.ShapeDtypeStruct(shape, dtype)


def load_kernel(parts, source, out, sems):
    rows = source.shape[0] // parts
    copies = []
    for k in range(parts):
        span = pl.ds(k * rows, rows)
        copy = pltpu.make_async_copy(source.at[span, :], out.at[span, :], sems.at[k])
        copy.start()
        copies.append(copy)
    for copy in copies:
        copy.wait()


def load(proj):
    parts = 16
    specs = [pl.BlockSpec(memory_space=pl.ANY)]
    scratch = [pltpu.SemaphoreType.DMA((parts,))]
    kernel = functools.partial(load_kernel, parts)
    return call(kernel, [proj], specs, array(proj.shape, proj.dtype), 20000000000, scratch)


def place_of(way, seq_len, seq_way):
    start = used = jnp.int32(0)
    for s in range(seq_len.shape[0]):
        start += jnp.where(seq_way[s] < way, seq_len[s], 0)
        used += jnp.where(seq_way[s] == way, seq_len[s], 0)
    return start, used


def hot_rows(rows, slots, start, used):
    row = lax.broadcasted_iota(I32, (rows, slots), 0)
    slot = lax.broadcasted_iota(I32, (rows, slots), 1)
    return (row - slot == start) & (slot < used)


def compact_kernel(seq_len, seq_way, _, *refs):
    pieces, out, mine = refs[:-2], refs[-2], refs[-1]
    rows, slots = out.shape[0], pieces[0].shape[0]
    half = mine.shape[0]
    dp = lax.axis_index("dp")
    spots = lax.axis_size("dp") // PAIR
    spot, core = dp // PAIR, dp % PAIR
    total = None
    for k in range(spots):
        there = lax.rem(spot + spots - k, spots) * PAIR
        for c, piece in zip((core, 1 - core), pieces[PAIR * k : PAIR * k + PAIR]):
            hot = hot_rows(rows, slots, *place_of(there + c, seq_len, seq_way))
            part = jnp.dot(jnp.where(hot, 1.0, 0.0).astype(BF16), piece[...], preferred_element_type=F32)
            total = part if total is None else total + part
    out[...] = total.astype(BF16)
    mine[...] = out[pl.ds(pl.multiple_of(core * half, half), half), :]


def target_kernel(seq_len, seq_way, _, ids, out):
    ways, slots = ids.shape
    rows = out.shape[0]
    total = jnp.zeros((rows, slots), I32)
    for way in range(ways):
        hot = hot_rows(rows, slots, *place_of(way, seq_len, seq_way))
        total += jnp.where(hot, ids[way : way + 1, :], 0)
    out[...] = jnp.broadcast_to(jnp.sum(total, axis=1, keepdims=True), out.shape)


def assemble(left, column, mine, other):
    half, depth = mine.shape
    core = lax.axis_index("dp") % PAIR
    left[pl.ds(pl.multiple_of(core * half, half), half), column : column + depth] = mine[...]
    left[pl.ds(pl.multiple_of((1 - core) * half, half), half), column : column + depth] = other[...]


def weights_of(proj, block, depth, n, wide):
    return proj[pl.ds(pl.multiple_of(block * depth, depth), depth), n : n + wide]


def first_kernel(left, proj, out):
    wide = min(512, out.shape[1])
    for n in range(0, out.shape[1], wide):
        weights = weights_of(proj, lax.axis_index("vocab"), left.shape[1], n, wide)
        out[:, n : n + wide] = jnp.dot(left[...], weights, preferred_element_type=F32)


def ring_block(j):
    vocab, size = lax.axis_index("vocab"), lax.axis_size("vocab")
    return lax.rem(vocab + size - PAIR * j, size)


def across(block):
    return block + 1 - PAIR * lax.rem(block, PAIR)


def block_kernel(j, ring_mine, ring_other, pair_mine, pair_other, proj, carry, out, left):
    depth = ring_mine.shape[1]
    assemble(left, 0, ring_mine, ring_other)
    assemble(left, depth, pair_mine, pair_other)
    wide = min(512, out.shape[1])
    for n in range(0, out.shape[1], wide):
        total = jnp.dot(
            left[:, :depth], weights_of(proj, ring_block(j), depth, n, wide), preferred_element_type=F32
        )
        total += jnp.dot(
            left[:, depth:], weights_of(proj, across(ring_block(j - 1)), depth, n, wide), preferred_element_type=F32
        )
        out[:, n : n + wide] = carry[:, n : n + wide] + total


def last_kernel(j, mine, other, proj, carry, targets, out, left, logits):
    rows, width = carry.shape
    depth = mine.shape[1]
    assemble(left, 0, mine, other)
    wide = min(512, width)
    for n in range(0, width, wide):
        weights = weights_of(proj, across(ring_block(j)), depth, n, wide)
        logits[:, n : n + wide] = carry[:, n : n + wide] + jnp.dot(left[...], weights, preferred_element_type=F32)
    first = (lax.axis_index("dp") * lax.axis_size("vocab") + lax.axis_index("vocab")) * width
    group = 16
    lane = lax.broadcasted_iota(I32, (group, LANES), 1)
    for r in range(0, rows, group):
        band = slice(r, r + group)
        peak = logits[band, :LANES]
        for n in range(LANES, width, LANES):
            peak = jnp.maximum(peak, logits[band, n : n + LANES])
        top = jnp.max(peak, axis=1, keepdims=True)
        wanted = targets[band, :] - first - lane
        total = moment = picked = jnp.zeros((group, LANES), F32)
        for n in range(0, width, LANES):
            value = logits[band, n : n + LANES]
            shifted = value - top
            weight = jnp.exp(shifted)
            total += weight
            moment += weight * shifted
            picked = jnp.where(wanted == n, value, picked)
        packed = jnp.where(lane == 0, top, 0.0)
        packed = jnp.where(lane == 1, jnp.sum(total, axis=1, keepdims=True), packed)
        packed = jnp.where(lane == 2, jnp.sum(moment, axis=1, keepdims=True), packed)
        packed = jnp.where(lane == 3, jnp.sum(picked, axis=1, keepdims=True), packed)
        logits[band, :LANES] = packed
    stats = jnp.transpose(logits[:, :LANES])[: out.shape[1], :]
    out[...] = jnp.broadcast_to(stats[None], out.shape)


def per_device(hidden, proj, target_ids, seq_len, seq_way):
    ways, size = lax.axis_size("dp"), lax.axis_size("vocab")
    slots, depth = hidden.shape
    width = proj.shape[1]
    spots, ring = ways // PAIR, size // PAIR
    kept = slots + (ways - 1) * (5 * slots // 16)
    rows = round_up(kept, 32)
    half = rows // 2

    def permute(value, axis, count, to):
        return lax.ppermute(value, axis, [(i, to(i)) for i in range(count)])

    def swap(value):
        return permute(value, "dp", ways, lambda i: i ^ 1)

    def over_pair(value):
        return permute(value, "vocab", size, lambda i: i ^ 1)

    def over_ring(value):
        return permute(value, "vocab", size, lambda i: (i + PAIR) % size)

    pieces = [hidden, swap(hidden)]
    for k in range(1, spots):
        turned = permute(hidden, "dp", ways, lambda i: (i + k * PAIR) % ways)
        pieces += [turned, swap(turned)]
    ids, proj = lax.optimization_barrier((target_ids.reshape(ways, slots), proj))
    held = load(proj)
    smem = [in_smem(), in_smem()]
    own, mine = call(
        compact_kernel,
        [seq_len, seq_way, held, *pieces],
        smem + [in_vmem()] * (len(pieces) + 1),
        (array((rows, depth), BF16), array((half, depth), BF16)),
        2 * rows * slots * ways * depth,
    )
    targets = call(
        target_kernel, [seq_len, seq_way, held, ids], smem + [in_vmem()] * 2, array((rows, LANES), I32), 1000000
    )
    flops = 2 * rows * depth * width
    carry = call(first_kernel, [own, held], [in_vmem()] * 2, array((rows, width), F32), flops)

    along = mine
    for j in range(1, ring + 1):
        beside = over_pair(along)
        if j == ring:
            break
        along = over_ring(along)
        lefts = [along, swap(along), beside, swap(beside)]
        carry = call(
            functools.partial(block_kernel, j),
            [*lefts, held, carry],
            [in_vmem()] * 6,
            array((rows, width), F32),
            2 * flops,
            [pltpu.VMEM((rows, 2 * depth), BF16)],
            {5: 0},
        )
    count = ways * size
    stats = call(
        functools.partial(last_kernel, ring - 1),
        [beside, swap(beside), held, carry, targets],
        [in_vmem()] * 5,
        array((count, 4, rows), F32),
        flops,
        [pltpu.VMEM((rows, depth), BF16), pltpu.VMEM((rows, width), F32)],
    )

    stats, seq_len, seq_way = lax.optimization_barrier((stats, seq_len, seq_way))
    every = lax.all_to_all(stats, AXES, 0, 0)
    top = jnp.max(every[:, 0], axis=0)
    drop = every[:, 0] - top[None]
    scale = jnp.exp(drop)
    total = jnp.sum(scale * every[:, 1], axis=0)
    moment = jnp.sum(scale * (every[:, 2] + every[:, 1] * drop), axis=0)
    picked = jnp.sum(every[:, 3], axis=0)
    log_total = jnp.log(total)
    logprob = picked - top - log_total
    entropy = log_total - moment / total

    order = jnp.arange(seq_len.shape[0], dtype=I32)
    ahead = (seq_way[None, :] < seq_way[:, None]) | (
        (seq_way[None, :] == seq_way[:, None]) & (order[None, :] < order[:, None])
    )
    begin = jnp.sum(jnp.where(ahead, seq_len[None, :], 0), axis=1)
    dp = lax.axis_index("dp")
    start = jnp.sum(jnp.where(seq_way < dp, seq_len, 0))
    used = jnp.arange(slots, dtype=I32) < jnp.sum(jnp.where(seq_way == dp, seq_len, 0))
    row = jnp.arange(rows, dtype=I32)
    inside = (row[None, :] >= begin[:, None]) & (row[None, :] < (begin + seq_len)[:, None])
    seq_logprob = jnp.sum(jnp.where(inside, logprob[None, :], 0.0), axis=1)

    def place(values):
        padded = jnp.concatenate([values, jnp.zeros((slots,), values.dtype)])
        return jnp.where(used, lax.dynamic_slice_in_dim(padded, start, slots), 0.0)

    return place(logprob), place(entropy), seq_logprob


def solution(mesh):
    placed = (P("dp", "vocab"), P(None, AXES), P(), P(), P())

    return jax.shard_map(per_device, mesh=mesh, in_specs=placed, out_specs=(P("dp"), P("dp"), P()), check_vma=False)
```

time: 253 us -> 103 us (0.41)
  blocking collectives: 79.2 us -> 0 us
  waiting for transfers between devices: 109 us -> 50.9 us
  Pallas kernels: 0 us -> 29.6 us
  matrix products: 19.6 us -> 0 us
  local copies, waits for them, and re-layouts: 18 us -> 0.77 us
  starting transfers between devices: 0.08 us -> 15.3 us
  between operations: 14.2 us -> 2.76 us
  other arithmetic: 13.1 us -> 3.03 us
    all_gather x2 -> x0, waiting for transfers between devices: 108 us -> none  [the longest x1 97.1 us: per_device(): piece = lax.all_gather(slot_rows, 'vocab', axis=1, tiled=True)]
    ppermute x0 -> x17, waiting for transfers between devices: none -> 45.4 us  [permute(): return lax.ppermute(value, axis, [(i, to(i)) for i in range(count)])]
    psum x1 -> x0, blocking collectives: 40.8 us -> none  [per_device(): lax.psum((partial_total, partial_moment, partial_pick), ('dp', 'vocab'))]
    pmax x1 -> x0, blocking collectives: 38.4 us -> none  [per_device(): top = lax.pmax(jnp.max(logits, axis=1), ('dp', 'vocab'))]
    pallas_call x0 -> x8, Pallas kernels: none -> 29.6 us  [call(): pl.pallas_call(kernel, in_specs=specs, out_specs=jax.tree.map(lambda _: i...]
    dot_general x2 -> x0, matrix products: 19.6 us -> none  [the longest x1 18.9 us: per_device(): jnp.dot(piece, weights_part, preferred_element_type=jnp.float32)]
    gather x4 -> x0, local copies, waits for them, and re-layouts: 16.3 us -> none  [the longest x1 5.01 us: per_device(): entropy = jnp.take(entropy, position)]
    ppermute x0 -> x17, starting transfers between devices: none -> 9.65 us  [permute(): return lax.ppermute(value, axis, [(i, to(i)) for i in range(count)])]
  transfers between devices with their start and end apart: 2 -> 18, of which waited for: 2 -> 8; matrix products, arithmetic and copies ran while one was open for 5% -> 2% of each run, Pallas kernels for 0% -> 24%
where the time goes in v1:
time: 103 us; the launch traced here: 102 us
  waiting for transfers between devices  50.9 us (49%)
  Pallas kernels  29.6 us (29%)
  starting transfers between devices  15.3 us (15%)
  other arithmetic  3.03 us (3%)
  between operations  2.76 us (3%)
    ppermute x17, waiting for transfers between devices, permute(): return lax.ppermute(value, axis, [(i, to(i)) for i in range(count)])  45.4 us
    pallas_call x8, Pallas kernels, call(): pl.pallas_call(kernel, in_specs=specs, out_specs=jax.tree.map(lambda _: i...  29.6 us
    ppermute x17, starting transfers between devices, permute(): return lax.ppermute(value, axis, [(i, to(i)) for i in range(count)])  9.65 us
    all_to_all x1, starting transfers between devices, per_device(): every = lax.all_to_all(stats, AXES, 0, 0)  5.65 us
    all_to_all x1, waiting for transfers between devices, per_device(): every = lax.all_to_all(stats, AXES, 0, 0)  5.47 us
  transfers between devices with their start and end apart: 18, of which 8 were waited for; matrix products, arithmetic and copies ran while one was open for 2% of the time, Pallas kernels for 24%

profile of v1, /device:TPU:0, one launch (start us, length us, event | category | flops | bytes accessed | tf_op | source)
XLA Modules:
  0.0 102.4 jit_solution(14138053786914468280)
XLA Ops:
  0.6 3.1 %collective-permute-start.1 = (bf16[192,1024]{1,0:T(8,128)(2,1)}, bf16[192,1024]{1,0:T(8,128)(2,1)S(1)}, u32[]{:S(2)}, u32[]{:S(2)}) collective-permute-start(bf16[192,1024]{1,0:T(8,128)(2,1)} %refs_0_.1), channel_id=1, source_target_pairs={{0,16},{8,24},{16,0},{24,8},{1,17},{9,25},{17,1},{25,9},{2,18},{10... | collective-permute-start | bytes 1179656 | tf_op jit(solution)/shard_map/ppermute | solution.py:195
  3.7 0.0 collective-permute-start
  3.7 0.8 reshape.24.ids
  4.5 0.0 copy-start
  4.5 0.0 copy-start.1
  4.5 0.0 copy-start.2
  4.5 8.6 %collective-permute-done.1.refs_2_ = bf16[192,1024]{1,0:T(8,128)(2,1)S(1)} collective-permute-done((bf16[192,1024]{1,0:T(8,128)(2,1)}, bf16[192,1024]{1,0:T(8,128)(2,1)S(1)}, u32[]{:S(2)}, u32[]{:S(2)}) %collective-permute-start.1) | collective-permute-done | bytes 393248 | tf_op jit(solution)/shard_map/ppermute | solution.py:195
  13.0 0.0 collective-permute-start.2
  13.0 10.8 %shard_map.76._.proj = bf16[8192,2048]{1,0:T(8,128)(2,1)S(1)} custom-call(bf16[8192,2048]{1,0:T(8,128)(2,1)} %source), custom_call_target="tpu_custom_call" | custom-call | flops 20000000000 | bytes 1000000 | tf_op jit(solution)/shard_map/pallas_call | solution.py:30
  23.8 0.0 collective-permute-done.refs_1_
  23.8 0.0 collective-permute-done.2.refs_3_
  23.8 0.0 copy-done
  23.8 0.0 copy-done.1
  23.8 0.0 copy-done.2
  23.8 1.6 %shard_map.77 = (bf16[384,1024]{1,0:T(8,128)(2,1)S(1)}, bf16[192,1024]{1,0:T(8,128)(2,1)S(1)}) custom-call(s32[16]{0:T(128)S(1)} %copy-done.2, s32[16]{0:T(128)S(1)} %copy-done.1, bf16[8192,2048]{1,0:T(8,128)(2,1)S(1)} %shard_map.76._.proj, bf16[192,1024]{1,0:T(8,128)(2,1)S(1)} %copy-done, bf16[192,1024]{1,0:T(8,128)(2,1)S(1)} %collective-permute-done.refs_1_, ...), custom_call_target="tpu_custom_call" | custom-call | flops 603979776 | bytes 1000000 | tf_op jit(solution)/shard_map/pallas_call | solution.py:30
  25.4 1.8 %collective-permute-start.3 = (bf16[192,1024]{1,0:T(8,128)(2,1)S(1)}, bf16[192,1024]{1,0:T(8,128)(2,1)S(1)}, u32[]{:S(2)}, u32[]{:S(2)}) collective-permute-start(bf16[192,1024]{1,0:T(8,128)(2,1)S(1)} %get-tuple-element.11), channel_id=1, source_target_pairs={{0,2},{1,3},{2,4},{3,5},{4,6},{5,7},{6,0},{7,1},{8,10},{9,11},{10,... | collective-permute-start | bytes 1179656 | tf_op jit(solution)/shard_map/ppermute | solution.py:195
  27.3 11.8 %collective-permute-done.3.ring_mine = bf16[192,1024]{1,0:T(8,128)(2,1)S(1)} collective-permute-done((bf16[192,1024]{1,0:T(8,128)(2,1)S(1)}, bf16[192,1024]{1,0:T(8,128)(2,1)S(1)}, u32[]{:S(2)}, u32[]{:S(2)}) %collective-permute-start.3) | collective-permute-done | bytes 393248 | tf_op jit(solution)/shard_map/ppermute | solution.py:195
  39.1 0.0 collective-permute-start.4
  39.1 1.5 %collective-permute-start.15 = (bf16[192,1024]{1,0:T(8,128)(2,1)S(1)}, bf16[192,1024]{1,0:T(8,128)(2,1)S(1)}, u32[]{:S(2)}, u32[]{:S(2)}) collective-permute-start(bf16[192,1024]{1,0:T(8,128)(2,1)S(1)} %get-tuple-element.11), channel_id=1, source_target_pairs={{0,1},{1,0},{2,3},{3,2},{4,5},{5,4},{6,7},{7,6},{8,9},{9,8},{10,11... | collective-permute-start | bytes 1179656 | tf_op jit(solution)/shard_map/ppermute | solution.py:195
  40.6 0.0 collective-permute-start.14
  40.6 0.5 collective-permute-start.12
  41.2 10.7 %collective-permute-done.4.ring_mine = bf16[192,1024]{1,0:T(8,128)(2,1)S(1)} collective-permute-done((bf16[192,1024]{1,0:T(8,128)(2,1)S(1)}, bf16[192,1024]{1,0:T(8,128)(2,1)S(1)}, u32[]{:S(2)}, u32[]{:S(2)}) %collective-permute-start.4) | collective-permute-done | bytes 393248 | tf_op jit(solution)/shard_map/ppermute | solution.py:195
  51.9 0.0 collective-permute-start.5
  51.9 0.0 collective-permute-done.15.pair_mine
  51.9 0.0 collective-permute-start.16
  51.9 1.3 %collective-permute-start.9 = (bf16[192,1024]{1,0:T(8,128)(2,1)S(1)}, bf16[192,1024]{1,0:T(8,128)(2,1)S(1)}, u32[]{:S(2)}, u32[]{:S(2)}) collective-permute-start(bf16[192,1024]{1,0:T(8,128)(2,1)S(1)} %collective-permute-done.4.ring_mine), channel_id=1, source_target_pairs={{0,1},{1,0},{2,3},{3,2},{4,5},{5,4},{6,7},{7,6},{8,9},{9,8},{10,11... | collective-permute-start | bytes 1179656 | tf_op jit(solution)/shard_map/ppermute | solution.py:195
  53.2 0.9 shard_map.82.targets
  54.2 0.0 collective-permute-done.14.ring_other
  54.2 0.2 collective-permute-start.11
  54.4 5.1 %collective-permute-done.12.pair_mine = bf16[192,1024]{1,0:T(8,128)(2,1)S(1)} collective-permute-done((bf16[192,1024]{1,0:T(8,128)(2,1)S(1)}, bf16[192,1024]{1,0:T(8,128)(2,1)S(1)}, u32[]{:S(2)}, u32[]{:S(2)}) %collective-permute-start.12) | collective-permute-done | bytes 393248 | tf_op jit(solution)/shard_map/ppermute | solution.py:195
  59.5 0.0 collective-permute-start.13
  59.5 4.3 %collective-permute-done.5.ring_mine = bf16[192,1024]{1,0:T(8,128)(2,1)S(1)} collective-permute-done((bf16[192,1024]{1,0:T(8,128)(2,1)S(1)}, bf16[192,1024]{1,0:T(8,128)(2,1)S(1)}, u32[]{:S(2)}, u32[]{:S(2)}) %collective-permute-start.5) | collective-permute-done | bytes 393248 | tf_op jit(solution)/shard_map/ppermute | solution.py:195
  63.8 1.1 %collective-permute-start.6 = (bf16[192,1024]{1,0:T(8,128)(2,1)S(1)}, bf16[192,1024]{1,0:T(8,128)(2,1)S(1)}, u32[]{:S(2)}, u32[]{:S(2)}) collective-permute-start(bf16[192,1024]{1,0:T(8,128)(2,1)S(1)} %collective-permute-done.5.ring_mine), channel_id=1, source_target_pairs={{0,1},{1,0},{2,3},{3,2},{4,5},{5,4},{6,7},{7,6},{8,9},{9,8},{10,11... | collective-permute-start | bytes 1179656 | tf_op jit(solution)/shard_map/ppermute | solution.py:195
  64.9 1.8 %shard_map.78.carry = f32[384,2048]{1,0:T(8,128)S(1)} custom-call(bf16[384,1024]{1,0:T(8,128)(2,1)S(1)} %get-tuple-element.12.left, bf16[8192,2048]{1,0:T(8,128)(2,1)S(1)} %shard_map.76._.proj), custom_call_target="tpu_custom_call" | custom-call | flops 1610612736 | bytes 1000000 | tf_op jit(solution)/shard_map/pallas_call | solution.py:30
  66.7 0.0 collective-permute-done.16.pair_other
  66.7 0.1 collective-permute-start.8
  66.8 1.2 %collective-permute-done.9.pair_mine = bf16[192,1024]{1,0:T(8,128)(2,1)S(1)} collective-permute-done((bf16[192,1024]{1,0:T(8,128)(2,1)S(1)}, bf16[192,1024]{1,0:T(8,128)(2,1)S(1)}, u32[]{:S(2)}, u32[]{:S(2)}) %collective-permute-start.9) | collective-permute-done | bytes 393248 | tf_op jit(solution)/shard_map/ppermute | solution.py:195
  68.0 0.0 collective-permute-start.10
  68.0 3.7 %shard_map.79.carry = f32[384,2048]{1,0:T(8,128)S(1)} custom-call(bf16[192,1024]{1,0:T(8,128)(2,1)S(1)} %collective-permute-done.3.ring_mine, bf16[192,1024]{1,0:T(8,128)(2,1)S(1)} %collective-permute-done.14.ring_other, bf16[192,1024]{1,0:T(8,128)(2,1)S(1)} %collective-permute-done.15.pair_mine, ...), custom_call_target="tpu_custom_call", output_to_operand_aliasing={{}: (5, {})} | custom-call | flops 3221225472 | bytes 1000000 | tf_op jit(solution)/shard_map/pallas_call | solution.py:30
  71.7 3.7 %collective-permute-done.6.mine = bf16[192,1024]{1,0:T(8,128)(2,1)S(1)} collective-permute-done((bf16[192,1024]{1,0:T(8,128)(2,1)S(1)}, bf16[192,1024]{1,0:T(8,128)(2,1)S(1)}, u32[]{:S(2)}, u32[]{:S(2)}) %collective-permute-start.6) | collective-permute-done | bytes 393248 | tf_op jit(solution)/shard_map/ppermute | solution.py:195
  75.4 0.0 collective-permute-start.7
  75.4 0.0 collective-permute-done.11.ring_other
  75.4 0.0 collective-permute-done.13.pair_other
  75.4 3.7 %shard_map.80.carry = f32[384,2048]{1,0:T(8,128)S(1)} custom-call(bf16[192,1024]{1,0:T(8,128)(2,1)S(1)} %collective-permute-done.4.ring_mine, bf16[192,1024]{1,0:T(8,128)(2,1)S(1)} %collective-permute-done.11.ring_other, bf16[192,1024]{1,0:T(8,128)(2,1)S(1)} %collective-permute-done.12.pair_mine, ...), custom_call_target="tpu_custom_call", output_to_operand_aliasing={{}: (5, {})} | custom-call | flops 3221225472 | bytes 1000000 | tf_op jit(solution)/shard_map/pallas_call | solution.py:30
  79.1 0.0 collective-permute-done.8.ring_other
  79.1 0.0 collective-permute-done.10.pair_other
  79.1 3.7 %shard_map.81.carry = f32[384,2048]{1,0:T(8,128)S(1)} custom-call(bf16[192,1024]{1,0:T(8,128)(2,1)S(1)} %collective-permute-done.5.ring_mine, bf16[192,1024]{1,0:T(8,128)(2,1)S(1)} %collective-permute-done.8.ring_other, bf16[192,1024]{1,0:T(8,128)(2,1)S(1)} %collective-permute-done.9.pair_mine, ...), custom_call_target="tpu_custom_call", output_to_operand_aliasing={{}: (5, {})} | custom-call | flops 3221225472 | bytes 1000000 | tf_op jit(solution)/shard_map/pallas_call | solution.py:30
  82.8 0.0 collective-permute-done.7.other
  82.9 3.4 %shard_map.83 = f32[32,4,384]{2,1,0:T(4,128)} custom-call(bf16[192,1024]{1,0:T(8,128)(2,1)S(1)} %collective-permute-done.6.mine, bf16[192,1024]{1,0:T(8,128)(2,1)S(1)} %collective-permute-done.7.other, bf16[8192,2048]{1,0:T(8,128)(2,1)S(1)} %shard_map.76._.proj, f32[384,2048]{1,0:T(8,128)S(1)} %shard_map.81.carry, s32[384,128]{1,0:T(8,128)S(1)} %shard_map.82.targets), custom_call_target="tpu_custom_call" | custom-call | flops 1610612736 | bytes 1000000 | tf_op jit(solution)/shard_map/pallas_call | solution.py:30
  86.2 5.7 %all-to-all-start = ((f32[32,4,384]{2,1,0:T(4,128)}), f32[32,4,384]{2,1,0:T(4,128)S(1)}, u32[]{:S(2)}, u32[]{:S(2)}) async-start(f32[32,4,384]{2,1,0:T(4,128)} %shard_map.83), calls=%async_computation | async-start | bytes 393216 | tf_op jit(solution)/shard_map/all_to_all | solution.py:253
  91.9 0.2 select_reduce_fusion.1
  92.1 0.7 fusion.8
  94.7 5.5 %all-to-all-done = f32[32,4,384]{2,1,0:T(4,128)S(1)} async-done(((f32[32,4,384]{2,1,0:T(4,128)}), f32[32,4,384]{2,1,0:T(4,128)S(1)}, u32[]{:S(2)}, u32[]{:S(2)}) %all-to-all-start) | async-done | bytes 196640 | tf_op jit(solution)/shard_map/all_to_all | solution.py:253
  100.2 0.2 fusion.10
  100.4 0.7 select_reduce_fusion
  101.1 1.3 %fusion.6 = (f32[192]{0:T(256)}, f32[192]{0:T(256)}) fusion(s32[]{:T(128)S(6)} %select_n.28, f32[384]{0:T(512)S(1)} %get-tuple-element.29, s32[]{:T(128)} %get-tuple-element.21, f32[384]{0:T(512)S(1)} %get-tuple-element.28), kind=kLoop, calls=%fused_computation.22 | loop fusion | flops 576 | bytes 4616 | tf_op jit(solution)/shard_map/jit(_where)/select_n | solution.py:278
  (2 shorter events, 0.0 us)
Async XLA Ops:
  0.6 12.4 %collective-permute-start.1 = (bf16[192,1024]{1,0:T(8,128)(2,1)}, bf16[192,1024]{1,0:T(8,128)(2,1)S(1)}, u32[]{:S(2)}, u32[]{:S(2)}) collective-permute-start(bf16[192,1024]{1,0:T(8,128)(2,1)} %refs_0_.1), channel_id=1, source_target_pairs={{0,16},{8,24},{16,0},{24,8},{1,17},{9,25},{17,1},{25,9},{2,18},{10... | collective-permute-start | bytes 1179656 | tf_op jit(solution)/shard_map/ppermute | solution.py:195
  3.7 20.1 %collective-permute-start = (bf16[192,1024]{1,0:T(8,128)(2,1)}, bf16[192,1024]{1,0:T(8,128)(2,1)S(1)}, u32[]{:S(2)}, u32[]{:S(2)}) collective-permute-start(bf16[192,1024]{1,0:T(8,128)(2,1)} %refs_0_.1), channel_id=1, source_target_pairs={{0,8},{8,0},{16,24},{24,16},{1,9},{9,1},{17,25},{25,17},{2,10},{10... | collective-permute-start | bytes 1179656 | tf_op jit(solution)/shard_map/ppermute | solution.py:195
  4.5 19.4 %copy-start = (bf16[192,1024]{1,0:T(8,128)(2,1)S(1)}, bf16[192,1024]{1,0:T(8,128)(2,1)}, u32[]{:S(2)}) copy-start(bf16[192,1024]{1,0:T(8,128)(2,1)} %refs_0_.1) | copy-start | bytes 1179652
  4.5 19.4 %copy-start.1 = (s32[16]{0:T(128)S(1)}, s32[16]{0:T(128)}, u32[]{:S(2)}) copy-start(s32[16]{0:T(128)} %seq_way.3) | copy-start | bytes 196
  4.5 19.4 %copy-start.2 = (s32[16]{0:T(128)S(1)}, s32[16]{0:T(128)}, u32[]{:S(2)}) copy-start(s32[16]{0:T(128)} %seq_len.3) | copy-start | bytes 196
  13.0 10.8 %collective-permute-start.2 = (bf16[192,1024]{1,0:T(8,128)(2,1)S(1)}, bf16[192,1024]{1,0:T(8,128)(2,1)S(1)}, u32[]{:S(2)}, u32[]{:S(2)}) collective-permute-start(bf16[192,1024]{1,0:T(8,128)(2,1)S(1)} %collective-permute-done.1.refs_2_), channel_id=1, source_target_pairs={{0,8},{8,0},{16,24},{24,16},{1,9},{9,1},{17,25},{25,17},{2,10},{10... | collective-permute-start | bytes 1179656 | tf_op jit(solution)/shard_map/ppermute | solution.py:195
  25.4 13.7 %collective-permute-start.3 = (bf16[192,1024]{1,0:T(8,128)(2,1)S(1)}, bf16[192,1024]{1,0:T(8,128)(2,1)S(1)}, u32[]{:S(2)}, u32[]{:S(2)}) collective-permute-start(bf16[192,1024]{1,0:T(8,128)(2,1)S(1)} %get-tuple-element.11), channel_id=1, source_target_pairs={{0,2},{1,3},{2,4},{3,5},{4,6},{5,7},{6,0},{7,1},{8,10},{9,11},{10,... | collective-permute-start | bytes 1179656 | tf_op jit(solution)/shard_map/ppermute | solution.py:195
  39.1 12.8 %collective-permute-start.4 = (bf16[192,1024]{1,0:T(8,128)(2,1)S(1)}, bf16[192,1024]{1,0:T(8,128)(2,1)S(1)}, u32[]{:S(2)}, u32[]{:S(2)}) collective-permute-start(bf16[192,1024]{1,0:T(8,128)(2,1)S(1)} %collective-permute-done.3.ring_mine), channel_id=1, source_target_pairs={{0,2},{1,3},{2,4},{3,5},{4,6},{5,7},{6,0},{7,1},{8,10},{9,11},{10,... | collective-permute-start | bytes 1179656 | tf_op jit(solution)/shard_map/ppermute | solution.py:195
  39.1 12.8 %collective-permute-start.15 = (bf16[192,1024]{1,0:T(8,128)(2,1)S(1)}, bf16[192,1024]{1,0:T(8,128)(2,1)S(1)}, u32[]{:S(2)}, u32[]{:S(2)}) collective-permute-start(bf16[192,1024]{1,0:T(8,128)(2,1)S(1)} %get-tuple-element.11), channel_id=1, source_target_pairs={{0,1},{1,0},{2,3},{3,2},{4,5},{5,4},{6,7},{7,6},{8,9},{9,8},{10,11... | collective-permute-start | bytes 1179656 | tf_op jit(solution)/shard_map/ppermute | solution.py:195
  40.6 13.6 %collective-permute-start.14 = (bf16[192,1024]{1,0:T(8,128)(2,1)S(1)}, bf16[192,1024]{1,0:T(8,128)(2,1)S(1)}, u32[]{:S(2)}, u32[]{:S(2)}) collective-permute-start(bf16[192,1024]{1,0:T(8,128)(2,1)S(1)} %collective-permute-done.3.ring_mine), channel_id=1, source_target_pairs={{0,8},{8,0},{16,24},{24,16},{1,9},{9,1},{17,25},{25,17},{2,10},{10... | collective-permute-start | bytes 1179656 | tf_op jit(solution)/shard_map/ppermute | solution.py:195
  40.6 18.9 %collective-permute-start.12 = (bf16[192,1024]{1,0:T(8,128)(2,1)S(1)}, bf16[192,1024]{1,0:T(8,128)(2,1)S(1)}, u32[]{:S(2)}, u32[]{:S(2)}) collective-permute-start(bf16[192,1024]{1,0:T(8,128)(2,1)S(1)} %collective-permute-done.3.ring_mine), channel_id=1, source_target_pairs={{0,1},{1,0},{2,3},{3,2},{4,5},{5,4},{6,7},{7,6},{8,9},{9,8},{10,11... | collective-permute-start | bytes 1179656 | tf_op jit(solution)/shard_map/ppermute | solution.py:195
  51.9 11.9 %collective-permute-start.5 = (bf16[192,1024]{1,0:T(8,128)(2,1)S(1)}, bf16[192,1024]{1,0:T(8,128)(2,1)S(1)}, u32[]{:S(2)}, u32[]{:S(2)}) collective-permute-start(bf16[192,1024]{1,0:T(8,128)(2,1)S(1)} %collective-permute-done.4.ring_mine), channel_id=1, source_target_pairs={{0,2},{1,3},{2,4},{3,5},{4,6},{5,7},{6,0},{7,1},{8,10},{9,11},{10,... | collective-permute-start | bytes 1179656 | tf_op jit(solution)/shard_map/ppermute | solution.py:195
  51.9 14.8 %collective-permute-start.16 = (bf16[192,1024]{1,0:T(8,128)(2,1)S(1)}, bf16[192,1024]{1,0:T(8,128)(2,1)S(1)}, u32[]{:S(2)}, u32[]{:S(2)}) collective-permute-start(bf16[192,1024]{1,0:T(8,128)(2,1)S(1)} %collective-permute-done.15.pair_mine), channel_id=1, source_target_pairs={{0,8},{8,0},{16,24},{24,16},{1,9},{9,1},{17,25},{25,17},{2,10},{10... | collective-permute-start | bytes 1179656 | tf_op jit(solution)/shard_map/ppermute | solution.py:195
  51.9 16.1 %collective-permute-start.9 = (bf16[192,1024]{1,0:T(8,128)(2,1)S(1)}, bf16[192,1024]{1,0:T(8,128)(2,1)S(1)}, u32[]{:S(2)}, u32[]{:S(2)}) collective-permute-start(bf16[192,1024]{1,0:T(8,128)(2,1)S(1)} %collective-permute-done.4.ring_mine), channel_id=1, source_target_pairs={{0,1},{1,0},{2,3},{3,2},{4,5},{5,4},{6,7},{7,6},{8,9},{9,8},{10,11... | collective-permute-start | bytes 1179656 | tf_op jit(solution)/shard_map/ppermute | solution.py:195
  54.2 21.2 %collective-permute-start.11 = (bf16[192,1024]{1,0:T(8,128)(2,1)S(1)}, bf16[192,1024]{1,0:T(8,128)(2,1)S(1)}, u32[]{:S(2)}, u32[]{:S(2)}) collective-permute-start(bf16[192,1024]{1,0:T(8,128)(2,1)S(1)} %collective-permute-done.4.ring_mine), channel_id=1, source_target_pairs={{0,8},{8,0},{16,24},{24,16},{1,9},{9,1},{17,25},{25,17},{2,10},{10... | collective-permute-start | bytes 1179656 | tf_op jit(solution)/shard_map/ppermute | solution.py:195
  59.5 15.8 %collective-permute-start.13 = (bf16[192,1024]{1,0:T(8,128)(2,1)S(1)}, bf16[192,1024]{1,0:T(8,128)(2,1)S(1)}, u32[]{:S(2)}, u32[]{:S(2)}) collective-permute-start(bf16[192,1024]{1,0:T(8,128)(2,1)S(1)} %collective-permute-done.12.pair_mine), channel_id=1, source_target_pairs={{0,8},{8,0},{16,24},{24,16},{1,9},{9,1},{17,25},{25,17},{2,10},{10... | collective-permute-start | bytes 1179656 | tf_op jit(solution)/shard_map/ppermute | solution.py:195
  63.8 11.6 %collective-permute-start.6 = (bf16[192,1024]{1,0:T(8,128)(2,1)S(1)}, bf16[192,1024]{1,0:T(8,128)(2,1)S(1)}, u32[]{:S(2)}, u32[]{:S(2)}) collective-permute-start(bf16[192,1024]{1,0:T(8,128)(2,1)S(1)} %collective-permute-done.5.ring_mine), channel_id=1, source_target_pairs={{0,1},{1,0},{2,3},{3,2},{4,5},{5,4},{6,7},{7,6},{8,9},{9,8},{10,11... | collective-permute-start | bytes 1179656 | tf_op jit(solution)/shard_map/ppermute | solution.py:195
  66.7 12.4 %collective-permute-start.8 = (bf16[192,1024]{1,0:T(8,128)(2,1)S(1)}, bf16[192,1024]{1,0:T(8,128)(2,1)S(1)}, u32[]{:S(2)}, u32[]{:S(2)}) collective-permute-start(bf16[192,1024]{1,0:T(8,128)(2,1)S(1)} %collective-permute-done.5.ring_mine), channel_id=1, source_target_pairs={{0,8},{8,0},{16,24},{24,16},{1,9},{9,1},{17,25},{25,17},{2,10},{10... | collective-permute-start | bytes 1179656 | tf_op jit(solution)/shard_map/ppermute | solution.py:195
  68.0 11.1 %collective-permute-start.10 = (bf16[192,1024]{1,0:T(8,128)(2,1)S(1)}, bf16[192,1024]{1,0:T(8,128)(2,1)S(1)}, u32[]{:S(2)}, u32[]{:S(2)}) collective-permute-start(bf16[192,1024]{1,0:T(8,128)(2,1)S(1)} %collective-permute-done.9.pair_mine), channel_id=1, source_target_pairs={{0,8},{8,0},{16,24},{24,16},{1,9},{9,1},{17,25},{25,17},{2,10},{10... | collective-permute-start | bytes 1179656 | tf_op jit(solution)/shard_map/ppermute | solution.py:195
  75.4 7.5 %collective-permute-start.7 = (bf16[192,1024]{1,0:T(8,128)(2,1)S(1)}, bf16[192,1024]{1,0:T(8,128)(2,1)S(1)}, u32[]{:S(2)}, u32[]{:S(2)}) collective-permute-start(bf16[192,1024]{1,0:T(8,128)(2,1)S(1)} %collective-permute-done.6.mine), channel_id=1, source_target_pairs={{0,8},{8,0},{16,24},{24,16},{1,9},{9,1},{17,25},{25,17},{2,10},{10... | collective-permute-start | bytes 1179656 | tf_op jit(solution)/shard_map/ppermute | solution.py:195
  86.2 13.9 %all-to-all-start = ((f32[32,4,384]{2,1,0:T(4,128)}), f32[32,4,384]{2,1,0:T(4,128)S(1)}, u32[]{:S(2)}, u32[]{:S(2)}) async-start(f32[32,4,384]{2,1,0:T(4,128)} %shard_map.83), calls=%async_computation | async-start | bytes 393216 | tf_op jit(solution)/shard_map/all_to_all | solution.py:253
